TPU v7x, 32 devices: a whole 2x2x4 slice. The times are simulated.
32 devices in a mesh: member: 2 (over y), tx: 4 (over z), ty: 4 (over x, core).
Axes of the slice: x: 2, y: 2, z: 4, core: 2. Of those that a mesh axis runs over, the one named last changes fastest.
Arguments:
- tracers: float32 [80, 3, 128, 512], P('member', None, 'tx', 'ty'), parts along dimension 0, may hold values from 0.05 to 2
- velocity: float32 [2, 3, 128, 512], P(None, None, 'tx', 'ty'), may hold values from -0.4 to 0.4
- land_mask: int32 [3, 128, 512], P(None, 'tx', 'ty'), may hold values 0 or 1
- sunlight: float32 [128, 512], P('tx', 'ty'), may hold values from 0.3 to 3
- growth_max: float32 [52], P('member'), parts along dimension 0, may hold values from 0.2 to 1.5
- half_sat: float32 [8, 26], P('member'), parts along dimension 0, may hold values from 0.05 to 1
- light_half: float32 [52], P('member'), parts along dimension 0, may hold values from 0.1 to 1
- graze_max: float32 [20], P('member'), parts along dimension 0, may hold values from 0.2 to 1.5
- graze_half: float32 [20], P('member'), parts along dimension 0, may hold values from 0.2 to 2
- palatable: int32 [20, 26], P('member'), parts along dimension 0, may hold values 0 or 1
- stoichiometry: float32 [4], replicated, may hold values from 0.05 to 1
Outputs:
- updated: float32 [80, 3, 128, 512], P('member', None, 'tx', 'ty'), parts along dimension 0
There are 2 independent parts, one for each index of `member`. A program takes and returns all parts, laid end to end along the dimension named above; an argument that names none is the same for every part. Nothing has to cross between parts.
All inputs are finite; a program needn't handle non-finite values. No bound on the sum of `land_mask` on one device may be relied on, other than what follows from the above.
Results may differ from a plain program's by a relative error of at most 0.000064.
Values sent between devices are 32-bit elements; how exact they have to be, the bound alone decides.
A program may use at most 64 MiB of HBM per device.

v0:
```python
import jax
import jax.numpy as jnp
from jax import lax
from jax.sharding import PartitionSpec as P

NNUT = 4
NPHY = 26


plankton_mortality = 0.05
grazer_mortality = 0.3
assimilation = 0.3
attenuation = 0.4


def extended(array, sides, width, wrap):
    for axis, dim in sides:
        size, length = (lax.axis_size(axis), array.shape[dim])
        up = [(i, (i + 1) % size) for i in range(size if wrap else size - 1)]
        down = [(j, i) for i, j in up]
        last = lax.slice_in_dim(array, length - width, length, axis=dim)
        first = lax.slice_in_dim(array, 0, width, axis=dim)
        before = lax.ppermute(last, axis, up)
        after = lax.ppermute(first, axis, down)
        array = jnp.concatenate([before, array, after], axis=dim)
    return array


def window(values, offset, amount, axis_dim):
    return lax.slice_in_dim(values, offset, offset + amount, axis=axis_dim)


def advect(padded, courant, wet_mask, axis_dim, length):
    face_count = length + 1
    far_left = window(padded, 0, face_count, axis_dim)
    near_left = window(padded, 1, face_count, axis_dim)
    near_right = window(padded, 2, face_count, axis_dim)
    far_right = window(padded, 3, face_count, axis_dim)
    opened = window(wet_mask, 1, face_count, axis_dim) * window(wet_mask, 2, face_count, axis_dim)
    transport = window(courant, 2, face_count, axis_dim) * opened
    face_flux = transport * (
        7.0 / 12.0 * (near_left + near_right) - 1.0 / 12.0 * (far_left + far_right)
    )
    face_flux = face_flux + jnp.abs(transport) * (1.0 / 12.0) * (
        far_right - 3.0 * near_right + 3.0 * near_left - far_left
    )
    centre = window(padded, 2, length, axis_dim)
    outflow = window(face_flux, 1, length, axis_dim) - window(face_flux, 0, length, axis_dim)
    spread = window(transport, 1, length, axis_dim) - window(transport, 0, length, axis_dim)
    return centre - outflow + centre * spread


def ecology(
    concentration,
    irradiance,
    growth_max,
    half_sat,
    light_half,
    graze_max,
    graze_half,
    palatable,
    stoichiometry,
):
    nutrients = concentration[:NNUT]
    phytoplankton = concentration[NNUT : NNUT + NPHY]
    zooplankton = concentration[NNUT + NPHY :]
    saturation = nutrients[:, None, :] / (nutrients[:, None, :] + half_sat[:, :, None])
    nutrient_limit = jnp.min(saturation, axis=0)
    light_limit = irradiance[None, :] / (irradiance[None, :] + light_half[:, None])
    growth = growth_max[:, None] * nutrient_limit * light_limit * phytoplankton
    prey_weights = palatable.astype(jnp.float32)
    available = jnp.dot(prey_weights, phytoplankton, precision=lax.Precision.HIGHEST)
    grazing_rate = graze_max[:, None] * zooplankton / (graze_half[:, None] + available)
    grazed = phytoplankton * jnp.dot(prey_weights.T, grazing_rate, precision=lax.Precision.HIGHEST)
    ingested = grazing_rate * available
    plankton_loss = plankton_mortality * phytoplankton
    grazer_loss = grazer_mortality * zooplankton * zooplankton
    phyto_change = growth - grazed - plankton_loss
    grazer_change = assimilation * ingested - grazer_loss
    recycled = (
        jnp.sum(plankton_loss, axis=0)
        + jnp.sum(grazer_loss, axis=0)
        + (1.0 - assimilation) * jnp.sum(ingested, axis=0)
        - jnp.sum(growth, axis=0)
    )
    nutrient_change = stoichiometry[:, None] * recycled[None, :]
    return jnp.concatenate([nutrient_change, phyto_change, grazer_change], axis=0)


def shards(
    tracers,
    velocity,
    land_mask,
    sunlight,
    growth_max,
    half_sat,
    light_half,
    graze_max,
    graze_half,
    palatable,
    stoichiometry,
):
    tracer_count = tracers.shape[0]
    along_count = tracers.shape[2]
    across_count = tracers.shape[3]
    wet_mask = land_mask.astype(jnp.float32)[None]
    stacked = jnp.concatenate([tracers, velocity, wet_mask], axis=0)
    padded = extended(stacked, (("tx", 2),), 2, True)
    after_along = advect(
        padded[:tracer_count],
        padded[tracer_count : tracer_count + 1],
        padded[tracer_count + 2 : tracer_count + 3],
        2,
        along_count,
    )
    second = jnp.concatenate([after_along, velocity[1:2], wet_mask], axis=0)
    across = extended(second, (("ty", 3),), 2, False)
    advected = advect(
        across[:tracer_count],
        across[tracer_count : tracer_count + 1],
        across[tracer_count + 1 : tracer_count + 2],
        3,
        across_count,
    )
    levels = lax.broadcasted_iota(jnp.float32, (tracers.shape[1], 1, 1), 0)
    irradiance = (sunlight[None] * jnp.exp(-attenuation * (levels + 0.5))).reshape(-1)
    tendency = ecology(
        tracers.reshape(tracer_count, -1),
        irradiance,
        growth_max,
        half_sat,
        light_half,
        graze_max,
        graze_half,
        palatable,
        stoichiometry,
    )
    return advected + wet_mask * tendency.reshape(tracers.shape)


def solution(mesh):
    return jax.shard_map(
        shards,
        mesh=mesh,
        in_specs=(
            P("member", None, "tx", "ty"),
            P(None, None, "tx", "ty"),
            P(None, "tx", "ty"),
            P("tx", "ty"),
            P("member"),
            P("member", None),
            P("member"),
            P("member"),
            P("member"),
            P("member", None),
            P(),
        ),
        out_specs=P("member", None, "tx", "ty"),
        check_vma=False,
    )
```

profile of v0, /device:TPU:1, one launch (start us, length us, event | category | flops | bytes accessed | tf_op | source)
XLA Modules:
  0.0 57.9 jit_solution(4100524613495818624)
XLA Ops:
  0.0 0.9 %fusion.21 = (f32[3,32,128]{2,1,0:T(8,128)S(1)}, f32[1,3,32,128]{3,2,1,0:T(8,128)S(1)}) fusion(s32[3,32,128]{2,1,0:T(8,128)} %param.13), kind=kLoop, calls=%fused_computation.52 | loop fusion | flops 12288 | bytes 147456 | tf_op jit(solution)/shard_map/convert_element_type | solution.py:106
  1.0 1.4 %pad_maximum_fusion.3 = (f32[43,3,2,128]{3,2,1,0:T(2,128)S(1)}, f32[43,3,2,128]{3,2,1,0:T(2,128)S(1)}) fusion(f32[1,3,32,128]{3,2,1,0:T(8,128)S(1)} %get-tuple-element.25, f32[2,3,32,128]{3,2,1,0:T(8,128)} %param.12, f32[40,3,32,128]{3,2,1,0:T(8,128)} %param.11), kind=kLoop, calls=%fused_computation.30 | loop fusion | flops 132096 | bytes 2377728 | tf_op jit(solution)/shard_map/concatenate | solution.py:107
  2.3 4.2 %collective-permute-start = (f32[43,3,2,128]{3,0,2,1:T(8,128)S(1)}, f32[43,3,2,128]{3,0,2,1:T(8,128)}, u32[]{:S(2)}, u32[]{:S(2)}) collective-permute-start(f32[43,3,2,128]{3,0,2,1:T(8,128)S(1)} %copy.31), channel_id=1, source_target_pairs={{4,0},{8,4},{12,8},{0,12},{5,1},{9,5},{13,9},{1,13},{6,2},{10,6},{... | collective-permute-start | bytes 396296 | tf_op jit(solution)/shard_map/ppermute | solution.py:24
  6.5 0.7 %copy.33 = f32[43,3,2,128]{3,0,2,1:T(8,128)} copy(f32[43,3,2,128]{3,2,1,0:T(2,128)S(1)} %get-tuple-element.13) | data formatting | bytes 264192 | tf_op jit(solution)/shard_map/slice | solution.py:21
  7.6 4.6 %fusion.3 = f32[26,12288]{1,0:T(8,128)S(1)} fusion(f32[4,26]{0,1:T(8,128)S(1)} %copy.39, f32[4,12288]{1,0:T(4,128)S(1)} %bitcast.58), kind=kLoop, calls=%fused_computation.5 | loop fusion | flops 3514368 | bytes 1474976 | tf_op jit(solution)/shard_map/reduce_min | solution.py:68
  12.1 0.3 copy.43
  12.6 0.6 %copy-done.6 = f32[32,128]{1,0:T(8,128)S(1)} copy-done((f32[32,128]{1,0:T(8,128)S(1)}, f32[32,128]{1,0:T(8,128)}, u32[]{:S(2)}) %copy-start.6) | copy-done | bytes 16408
  13.2 0.6 multiply_reduce_fusion.1
  14.0 0.9 %copy.41 = f32[4,8,96,128]{3,1,2,0:T(8,128)S(1)} copy(f32[4,8,96,128]{3,2,1,0:T(8,128)S(1)} %bitcast.48) | data formatting | bytes 3145728
  15.0 0.5 copy.40
  15.6 1.2 %multiply_reduce_fusion.2 = (f32[12288]{0:T(1024)S(1)}, f32[10,12288]{1,0:T(8,128)S(1)}, f32[10,12288]{1,0:T(8,128)S(1)}) fusion(f32[10]{0:T(128)S(1)} %copy-done.12, f32[10,12288]{1,0:T(8,128)S(1)} %bitcast.59, f32[10]{0:T(128)S(1)} %copy-done.13, f32[26,12288]{1,0:T(8,128)S(1)} %bitcast.54, s32[10,26]{1,0:T(8,128)S(1)} %copy-done.11), kind=kOutput, calls=%fused_computation.28 | convolution fusion | flops 39432452 | bytes 2802784 | tf_op jit(solution)/shard_map/dot_general | solution.py:72
  16.9 3.2 %fusion.2 = f32[26,12288]{1,0:T(8,128)} fusion(f32[26,12288]{1,0:T(8,128)S(1)} %bitcast.55, f32[26,12288]{1,0:T(8,128)S(1)} %fusion.3, f32[26]{0:T(128)S(1)} %copy-done.9, f32[12288]{0:T(1024)S(1)} %bitcast.61, f32[26]{0:T(128)S(1)} %copy-done.10, s32[10,26]{1,0:T(8,128)S(1)} %copy-done.11, f32[10,12288]{1,0:T(8,128)S(1)} %get-tuple-element.26, ...), kind=kOutput, calls=%fused_computation.3 | convolution fusion | flops 41582852 | bytes 4867376 | tf_op jit(solution)/shard_map/dot_general | solution.py:74
  20.2 1.0 %copy.32 = f32[43,3,2,128]{3,2,1,0:T(2,128)S(1)} copy(f32[43,3,2,128]{3,0,2,1:T(8,128)} %collective-permute-done) | data formatting | bytes 264192 | tf_op jit(solution)/shard_map/ppermute | solution.py:24
  21.2 1.0 %copy.34 = f32[43,3,2,128]{3,2,1,0:T(2,128)S(1)} copy(f32[43,3,2,128]{3,0,2,1:T(8,128)} %collective-permute-done.1) | data formatting | bytes 264192 | tf_op jit(solution)/shard_map/ppermute | solution.py:23
  22.2 0.5 maximum_maximum_fusion.1
  22.7 1.6 %multiply_add_fusion.1 = f32[40,3,33,128]{3,2,1,0:T(8,128)S(1)} fusion(f32[43,3,34,128]{3,2,1,0:T(8,128)S(1)} %get-tuple-element.12, f32[43,3,34,128]{3,2,1,0:T(8,128)S(1)} %get-tuple-element.11, f32[3,33,128]{2,1,0:T(8,128)S(1)} %get-tuple-element.9, f32[3,33,128]{2,1,0:T(8,128)S(1)} %bitcast.57), kind=kLoop, calls=%fused_computation.11 | loop fusion | flops 6589440 | bytes 10238976 | tf_op jit(solution)/shard_map/add | solution.py:44
  24.4 0.4 fusion.8
  25.0 2.7 %fusion.20 = (f32[42,3,32,2]{3,2,1,0:T(8,128)}, f32[42,3,32,2]{3,2,1,0:T(8,128)}) fusion(f32[42,3,32,128]{3,2,1,0:T(8,128)S(1)} %pad_maximum_fusion.2), kind=kLoop, calls=%fused_computation.51 | loop fusion | bytes 129024 | tf_op jit(solution)/shard_map/slice | solution.py:21
  27.6 2.7 %copy.35 = f32[42,3,32,2]{0,2,3,1:T(8,128)S(1)} copy(f32[42,3,32,2]{3,2,1,0:T(8,128)} %get-tuple-element.18) | data formatting | bytes 64512 | tf_op jit(solution)/shard_map/slice | solution.py:22
  30.4 2.9 %collective-permute-start.2 = (f32[42,3,32,2]{0,2,3,1:T(8,128)S(1)}, f32[42,3,32,2]{0,2,3,1:T(8,128)S(1)}, u32[]{:S(2)}, u32[]{:S(2)}) collective-permute-start(f32[42,3,32,2]{0,2,3,1:T(8,128)S(1)} %copy.35), channel_id=1, source_target_pairs={{1,0},{2,1},{3,2},{5,4},{6,5},{7,6},{9,8},{10,9},{11,10},{13,12},{... | collective-permute-start | bytes 96776 | tf_op jit(solution)/shard_map/ppermute | solution.py:24
  33.2 2.7 %copy.37 = f32[42,3,32,2]{0,2,3,1:T(8,128)S(1)} copy(f32[42,3,32,2]{3,2,1,0:T(8,128)} %get-tuple-element.17) | data formatting | bytes 64512 | tf_op jit(solution)/shard_map/slice | solution.py:21
  36.0 3.0 %collective-permute-start.3 = (f32[42,3,32,2]{0,2,3,1:T(8,128)S(1)}, f32[42,3,32,2]{0,2,3,1:T(8,128)S(1)}, u32[]{:S(2)}, u32[]{:S(2)}) collective-permute-start(f32[42,3,32,2]{0,2,3,1:T(8,128)S(1)} %copy.37), channel_id=1, source_target_pairs={{0,1},{1,2},{2,3},{4,5},{5,6},{6,7},{8,9},{9,10},{10,11},{12,13},{... | collective-permute-start | bytes 96776 | tf_op jit(solution)/shard_map/ppermute | solution.py:23
  39.0 1.7 %maximum_bitcast_fusion = f32[5,8,96,128]{3,1,2,0:T(8,128)S(1)} fusion(f32[10,12288]{1,0:T(8,128)S(1)} %get-tuple-element.23, f32[26,12288]{1,0:T(8,128)} %fusion.2, f32[4,12288]{1,0:T(4,128)S(1)} %broadcast_multiply_fusion), kind=kLoop, calls=%fused_computation.20 | loop fusion | flops 983040 | bytes 3932160
  40.7 1.6 %copy.44 = f32[5,8,96,128]{3,2,1,0:T(8,128)} copy(f32[5,8,96,128]{3,1,2,0:T(8,128)S(1)} %maximum_bitcast_fusion) | data formatting | bytes 3932160
  42.3 3.0 %copy.36 = f32[42,3,32,2]{3,2,1,0:T(8,128)} copy(f32[42,3,32,2]{0,2,3,1:T(8,128)S(1)} %collective-permute-done.2) | data formatting | bytes 64512 | tf_op jit(solution)/shard_map/ppermute | solution.py:24
  45.3 3.0 %copy.38 = f32[42,3,32,2]{3,2,1,0:T(8,128)} copy(f32[42,3,32,2]{0,2,3,1:T(8,128)S(1)} %collective-permute-done.3) | data formatting | bytes 64512 | tf_op jit(solution)/shard_map/ppermute | solution.py:23
  48.4 1.1 %multiply_bitcast_fusion = (f32[3,32,129]{2,1,0:T(8,128)S(1)}, f32[1,3,32,129]{3,2,1,0:T(8,128)S(1)}) fusion(f32[42,3,32,2]{3,2,1,0:T(8,128)} %copy.36, f32[1,3,32,128]{3,2,1,0:T(8,128)S(1)} %get-tuple-element.25, f32[1,3,32,128]{3,2,1,0:T(8,128)S(1)} %slice.150, f32[40,3,32,128]{3,2,1,0:T(8,128)S(1)} %fusion.8, f32[42,3,32,2]{3,2,1,0:T(8,128)} %copy.38), kind=kLoop, calls=%fused_computation.36 | loop fusion | flops 160992 | bytes 2227968 | tf_op jit(solution)/shard_map/mul | solution.py:44
  49.5 0.5 copy-done.2
  50.0 0.6 %copy-done.3 = f32[42,3,32,2]{3,2,1,0:T(8,128)S(1)} copy-done((f32[42,3,32,2]{3,2,1,0:T(8,128)S(1)}, f32[42,3,32,2]{3,2,1,0:T(8,128)}, u32[]{:S(2)}) %copy-start.3) | copy-done | bytes 32280
  50.6 2.6 %maximum_maximum_fusion = (f32[42,3,32,130]{3,2,1,0:T(8,128)S(1)}, f32[42,3,32,130]{3,2,1,0:T(8,128)S(1)}) fusion(f32[1,3,32,128]{3,2,1,0:T(8,128)S(1)} %get-tuple-element.25, f32[1,3,32,128]{3,2,1,0:T(8,128)S(1)} %slice.150, f32[40,3,32,128]{3,2,1,0:T(8,128)S(1)} %fusion.8, f32[42,3,32,2]{3,2,1,0:T(8,128)S(1)} %copy-done.3, f32[42,3,32,2]{3,2,1,0:T(8,128)S(1)} %copy-done.2), kind=kLoop, calls=%fused_computation.7 | loop fusion | flops 3144960 | bytes 6322176 | tf_op jit(solution)/shard_map/concatenate | solution.py:25
  53.3 2.5 %multiply_add_fusion = f32[40,3,32,129]{3,2,1,0:T(8,128)S(1)} fusion(f32[42,3,32,130]{3,2,1,0:T(8,128)S(1)} %get-tuple-element.16, f32[42,3,32,130]{3,2,1,0:T(8,128)S(1)} %get-tuple-element.15, f32[3,32,129]{2,1,0:T(8,128)S(1)} %get-tuple-element.7, f32[3,32,129]{2,1,0:T(8,128)S(1)} %bitcast.56), kind=kLoop, calls=%fused_computation.8 | loop fusion | flops 6439680 | bytes 10006272 | tf_op jit(solution)/shard_map/add | solution.py:44
  55.8 2.1 %fusion.6 = f32[40,3,32,128]{3,2,1,0:T(8,128)} fusion(f32[40,3,32,128]{3,2,1,0:T(8,128)S(1)} %fusion.8, f32[40,3,32,129]{3,2,1,0:T(8,128)S(1)} %multiply_add_fusion, f32[40,3,32,128]{3,2,1,0:T(8,128)S(1)} %bitcast.46, f32[3,32,128]{2,1,0:T(8,128)S(1)} %get-tuple-element.24, f32[3,32,128]{2,1,0:T(8,128)S(1)} %fusion.13), kind=kLoop, calls=%fused_computation.16 | loop fusion | flops 2949120 | bytes 9928704 | tf_op jit(solution)/shard_map/add | solution.py:138
  (49 shorter events, 1.3 us)
Async XLA Ops:
  0.0 7.2 %copy-start = (f32[40,3,32,128]{3,2,1,0:T(8,128)S(1)}, f32[40,3,32,128]{3,2,1,0:T(8,128)}, u32[]{:S(2)}) copy-start(f32[40,3,32,128]{3,2,1,0:T(8,128)} %param.11) | copy-start | bytes 5898244
  1.0 6.4 %slice-start = ((f32[40,3,32,128]{3,2,1,0:T(8,128)}), f32[4,3,32,128]{3,2,1,0:T(8,128)S(1)}, s32[]{:S(2)}) async-start(f32[40,3,32,128]{3,2,1,0:T(8,128)} %param.11), calls=%async_computation | async-start | bytes 393216 | tf_op jit(solution)/shard_map/slice | solution.py:64
  1.0 6.5 %copy-start.7 = (f32[4,26]{1,0:T(4,128)S(1)}, f32[4,26]{1,0:T(4,128)}, u32[]{:S(2)}) copy-start(f32[4,26]{1,0:T(4,128)} %param.16) | copy-start | bytes 1252
  2.3 17.8 %collective-permute-start = (f32[43,3,2,128]{3,0,2,1:T(8,128)S(1)}, f32[43,3,2,128]{3,0,2,1:T(8,128)}, u32[]{:S(2)}, u32[]{:S(2)}) collective-permute-start(f32[43,3,2,128]{3,0,2,1:T(8,128)S(1)} %copy.31), channel_id=1, source_target_pairs={{4,0},{8,4},{12,8},{0,12},{5,1},{9,5},{13,9},{1,13},{6,2},{10,6},{... | collective-permute-start | bytes 396296 | tf_op jit(solution)/shard_map/ppermute | solution.py:24
  7.2 13.9 %collective-permute-start.1 = (f32[43,3,2,128]{3,0,2,1:T(8,128)}, f32[43,3,2,128]{3,0,2,1:T(8,128)}, u32[]{:S(2)}, u32[]{:S(2)}) collective-permute-start(f32[43,3,2,128]{3,0,2,1:T(8,128)} %copy.33), channel_id=1, source_target_pairs={{0,4},{4,8},{8,12},{12,0},{1,5},{5,9},{9,13},{13,1},{2,6},{6,10},{... | collective-permute-start | bytes 396296 | tf_op jit(solution)/shard_map/ppermute | solution.py:23
  12.4 0.7 %copy-start.6 = (f32[32,128]{1,0:T(8,128)S(1)}, f32[32,128]{1,0:T(8,128)}, u32[]{:S(2)}) copy-start(f32[32,128]{1,0:T(8,128)} %param.14) | copy-start | bytes 49156
  12.4 0.8 %copy-start.9 = (f32[26]{0:T(128)S(1)}, f32[26]{0:T(128)}, u32[]{:S(2)}) copy-start(f32[26]{0:T(128)} %param.17) | copy-start | bytes 316
  12.5 0.8 %copy-start.10 = (f32[26]{0:T(128)S(1)}, f32[26]{0:T(128)}, u32[]{:S(2)}) copy-start(f32[26]{0:T(128)} %param.15) | copy-start | bytes 316
  14.9 0.7 %copy-start.11 = (s32[10,26]{1,0:T(8,128)S(1)}, s32[10,26]{1,0:T(8,128)}, u32[]{:S(2)}) copy-start(s32[10,26]{1,0:T(8,128)} %param.20) | copy-start | bytes 3124
  14.9 0.7 %copy-start.12 = (f32[10]{0:T(128)S(1)}, f32[10]{0:T(128)}, u32[]{:S(2)}) copy-start(f32[10]{0:T(128)} %param.19) | copy-start | bytes 124
  14.9 0.7 %copy-start.13 = (f32[10]{0:T(128)S(1)}, f32[10]{0:T(128)}, u32[]{:S(2)}) copy-start(f32[10]{0:T(128)} %param.18) | copy-start | bytes 124
  15.6 1.2 %copy-start.8 = (f32[4]{0:T(128)S(1)}, f32[4]{0:T(128)}, u32[]{:S(2)}) copy-start(f32[4]{0:T(128)} %param.21) | copy-start | bytes 52
  16.9 3.2 %copy-start.5 = (f32[2,3,32,128]{3,2,1,0:T(8,128)S(1)}, f32[2,3,32,128]{3,2,1,0:T(8,128)}, u32[]{:S(2)}) copy-start(f32[2,3,32,128]{3,2,1,0:T(8,128)} %param.12) | copy-start | bytes 294916
  22.7 1.6 %copy-start.1 = (f32[40,3,32,128]{3,2,1,0:T(8,128)S(1)}, f32[40,3,32,128]{3,2,1,0:T(8,128)}, u32[]{:S(2)}) copy-start(f32[40,3,32,128]{3,2,1,0:T(8,128)} %param.11) | copy-start | bytes 5898244
  30.4 11.9 %collective-permute-start.2 = (f32[42,3,32,2]{0,2,3,1:T(8,128)S(1)}, f32[42,3,32,2]{0,2,3,1:T(8,128)S(1)}, u32[]{:S(2)}, u32[]{:S(2)}) collective-permute-start(f32[42,3,32,2]{0,2,3,1:T(8,128)S(1)} %copy.35), channel_id=1, source_target_pairs={{1,0},{2,1},{3,2},{5,4},{6,5},{7,6},{9,8},{10,9},{11,10},{13,12},{... | collective-permute-start | bytes 96776 | tf_op jit(solution)/shard_map/ppermute | solution.py:24
  36.0 9.3 %collective-permute-start.3 = (f32[42,3,32,2]{0,2,3,1:T(8,128)S(1)}, f32[42,3,32,2]{0,2,3,1:T(8,128)S(1)}, u32[]{:S(2)}, u32[]{:S(2)}) collective-permute-start(f32[42,3,32,2]{0,2,3,1:T(8,128)S(1)} %copy.37), channel_id=1, source_target_pairs={{0,1},{1,2},{2,3},{4,5},{5,6},{6,7},{8,9},{9,10},{10,11},{12,13},{... | collective-permute-start | bytes 96776 | tf_op jit(solution)/shard_map/ppermute | solution.py:23
  48.4 1.6 %copy-start.2 = (f32[42,3,32,2]{3,2,1,0:T(8,128)S(1)}, f32[42,3,32,2]{3,2,1,0:T(8,128)}, u32[]{:S(2)}) copy-start(f32[42,3,32,2]{3,2,1,0:T(8,128)} %copy.36) | copy-start | bytes 96772
  48.4 2.3 %copy-start.3 = (f32[42,3,32,2]{3,2,1,0:T(8,128)S(1)}, f32[42,3,32,2]{3,2,1,0:T(8,128)}, u32[]{:S(2)}) copy-start(f32[42,3,32,2]{3,2,1,0:T(8,128)} %copy.38) | copy-start | bytes 96772
  53.3 2.5 %copy-start.4 = (f32[5,8,96,128]{3,2,1,0:T(8,128)S(1)}, f32[5,8,96,128]{3,2,1,0:T(8,128)}, u32[]{:S(2)}) copy-start(f32[5,8,96,128]{3,2,1,0:T(8,128)} %copy.44) | copy-start | bytes 5898244
where the time goes:
time: 58.3 us; the launch traced here: 57.9 us
  local copies, waits for them, and re-layouts  22.6 us (39%)
  other arithmetic  20.5 us (35%)
  starting transfers between devices  10.1 us (17%)
  matrix products  4.4 us (8%)
    ppermute x2, starting transfers between devices, extended(): after = lax.ppermute(first, axis, down)  7.04 us
    slice x3, local copies, waits for them, and re-layouts, extended(): last = lax.slice_in_dim(array, length - width, length, axis=dim)  6.08 us
    unnamed x37, local copies, waits for them, and re-layouts  5.74 us
    reduce_min x1, other arithmetic, ecology(): nutrient_limit = jnp.min(saturation, axis=0)  4.58 us
    add x2, other arithmetic, advect(): face_flux + jnp.abs(transport) * (1.0 / 12.0) * (far_right - 3.0 * near_r...  4.1 us
    ppermute x2, local copies, waits for them, and re-layouts, extended(): before = lax.ppermute(last, axis, up)  4.02 us
    ppermute x2, local copies, waits for them, and re-layouts, extended(): after = lax.ppermute(first, axis, down)  4.01 us
    dot_general x1, matrix products, ecology(): jnp.dot(prey_weights.T, grazing_rate, precision=lax.Precision.HIGHEST)  3.21 us
  transfers between devices with their start and end apart: 4, of which 0 were waited for; matrix products, arithmetic and copies ran while one was open for 39% of the time, Pallas kernels for 0%

commit v1 on v0

v1 whole, which is shorter than its diff:
```python
import functools

import jax
import jax.numpy as jnp
from jax import lax
from jax.experimental import pallas as pl
from jax.experimental.pallas import tpu as pltpu
from jax.sharding import PartitionSpec as P

NNUT = 4
plankton_mortality = 0.05
grazer_mortality = 0.3
assimilation = 0.3
attenuation = 0.4

ROWS = 8
LANES = 128
FIRST = 8
GROUP = 4
PER = LANES // GROUP
MESH = pl.DeviceIdType.MESH


def stencil_weights(here, after):
    hp, hm = jnp.maximum(here, 0.0), jnp.minimum(here, 0.0)
    ap, am = jnp.maximum(after, 0.0), jnp.minimum(after, 0.0)
    sixth = 1.0 / 6.0
    return (
        -sixth * hp,
        5.0 * sixth * hp + 2.0 * sixth * hm + sixth * ap,
        1.0 - 4.0 * sixth * hp - sixth * hm + sixth * ap + 4.0 * sixth * am,
        -sixth * hm - 2.0 * sixth * ap - 5.0 * sixth * am,
        sixth * am,
    )


def exchange_kernel(
    dims,
    tracers,
    velocity,
    land_mask,
    sunlight,
    growth_max,
    half_sat,
    light_half,
    graze_max,
    graze_half,
    palatable,
    stoichiometry,
    swept,
    tend,
    halo,
    pad,
    mask_buf,
    sun_buf,
    send_lo,
    send_hi,
    recv_lo,
    recv_hi,
    pack_in,
    pack_out,
    left_in,
    left_out,
    right_in,
    right_out,
    prey,
    load_sems,
    row_sems,
    col_sems,
):
    count, levels, along, nphy, nzoo = dims
    fields = count + 2
    tiles = along // ROWS
    inner = tiles - 2
    last = FIRST + along - ROWS
    tx_size, ty_size = lax.axis_size("tx"), lax.axis_size("ty")
    tx, ty = lax.axis_index("tx"), lax.axis_index("ty")
    up, down = lax.rem(tx + 1, tx_size), lax.rem(tx + tx_size - 1, tx_size)
    right, left = lax.rem(ty + 1, ty_size), lax.rem(ty + ty_size - 1, ty_size)

    def load(slot, src, dst):
        copy = pltpu.make_async_copy(src, dst, load_sems.at[slot])
        copy.start()
        return copy

    own = pl.ds(0, count)
    loads = [
        load(0, land_mask, mask_buf),
        load(1, velocity.at[0], pad.at[count, :, pl.ds(FIRST, along), :]),
        load(2, tracers.at[:, :, pl.ds(0, ROWS), :], pad.at[own, :, pl.ds(FIRST, ROWS), :]),
        load(3, tracers.at[:, :, pl.ds(along - ROWS, ROWS), :], pad.at[own, :, pl.ds(last, ROWS), :]),
        load(4, tracers.at[:, :, pl.ds(ROWS, along - 2 * ROWS), :],
             pad.at[own, :, pl.ds(FIRST + ROWS, along - 2 * ROWS), :]),
        load(5, velocity.at[1], pad.at[count + 2, :, pl.ds(FIRST, along), :]),
        load(6, sunlight, sun_buf),
    ]

    barrier = pltpu.get_barrier_semaphore()
    for target in ({"tx": up}, {"tx": down}, {"ty": right}, {"ty": left}):
        pl.semaphore_signal(barrier, inc=1, device_id=target, device_id_type=MESH)

    def to_float(z, carry):
        for k in range(nphy):
            prey[z, k] = palatable[z, k].astype(jnp.float32)
        return carry

    lax.fori_loop(0, nzoo, to_float, 0)

    loads[0].wait()
    pad[count + 1, :, FIRST:FIRST + along, :] = mask_buf[...].astype(jnp.float32)
    for slot in (1, 2, 3):
        loads[slot].wait()
    send_lo[...] = pad[0:fields, :, FIRST:FIRST + 2, :]
    send_hi[...] = pad[0:fields, :, FIRST + along - 2:FIRST + along, :]

    pl.semaphore_wait(barrier, 4)

    def remote(src, dst, sems, slot, target):
        return pltpu.make_async_remote_copy(
            src_ref=src, dst_ref=dst, send_sem=sems.at[slot, 0], recv_sem=sems.at[slot, 1],
            device_id=target, device_id_type=MESH,
        )

    to_down = remote(send_lo, recv_hi, row_sems, 0, {"tx": down})
    to_up = remote(send_hi, recv_lo, row_sems, 1, {"tx": up})
    to_down.start()
    to_up.start()
    for slot in (4, 5, 6):
        loads[slot].wait()

    lane_group = lax.broadcasted_iota(jnp.int32, (ROWS, LANES), 1) // GROUP

    def sweep(level, tile, pack, spot):
        base = FIRST + tile * ROWS

        def at(field, shift):
            return pad[field, level, pl.ds(base + shift, ROWS), :]

        wet = at(count + 1, 0)
        here = at(count, 0) * at(count + 1, -1) * wet
        after = at(count, 1) * wet * at(count + 1, 1)
        weights = stencil_weights(here, after)
        packed = [None] * (-(-fields // PER))
        for field in range(fields):
            if field < count:
                value = at(field, -2) * weights[0]
                for shift in range(-1, 3):
                    value = value + at(field, shift) * weights[shift + 2]
            elif field == count:
                value = at(count + 2, 0)
            else:
                value = wet
            swept[field, level, pl.ds(tile * ROWS, ROWS), :] = value
            group, place = divmod(field, PER)
            turned = pltpu.roll(value, (GROUP * place + 2) % LANES, 1)
            if place == 0:
                packed[group] = turned
            else:
                packed[group] = jnp.where(lane_group == place, turned, packed[group])
        for group, value in enumerate(packed):
            pack[level, spot, group] = value

    def sides(slot, pack, from_left, from_right):
        to_right = remote(pack, from_left, col_sems, slot, {"ty": right})
        to_left = remote(pack, from_right, col_sems, slot + 1, {"ty": left})
        return to_right, to_left

    has_left, has_right = ty > 0, ty < ty_size - 1

    def start(pair):
        pl.when(has_right)(pair[0].start)
        pl.when(has_left)(pair[1].start)

    def inner_level(level, carry):
        for tile in range(1, tiles - 1):
            sweep(level, tile, pack_in, tile - 1)
        return carry

    lax.fori_loop(0, levels, inner_level, 0)
    early = sides(0, pack_in, left_in, right_in)
    start(early)

    def ecology(level, carry):
        def field(index):
            return pad[index, level, pl.ds(FIRST, along), :]

        wet = field(count + 1)
        depth = jnp.full((along, LANES), -attenuation * (level.astype(jnp.float32) + 0.5), jnp.float32)
        light = sun_buf[...] * jnp.exp(depth)
        inverse = [1.0 / field(j) for j in range(NNUT)]
        recycled = jnp.zeros((along, LANES), jnp.float32)
        for k in range(nphy):
            phyto = field(NNUT + k)
            worst = inverse[0] * half_sat[0, k]
            for j in range(1, NNUT):
                worst = jnp.maximum(worst, inverse[j] * half_sat[j, k])
            growth = growth_max[k] * light * phyto / ((1.0 + worst) * (light + light_half[k]))
            loss = plankton_mortality * phyto
            change = growth - loss
            recycled = recycled - change
            tend[NNUT + k, level] = change
        available = [None] * nzoo
        for k in range(nphy):
            phyto = field(NNUT + k)
            for z in range(nzoo):
                term = prey[z, k] * phyto
                available[z] = term if k == 0 else available[z] + term
        rates = []
        for z in range(nzoo):
            zoo = field(NNUT + nphy + z)
            rate = graze_max[z] * zoo / (graze_half[z] + available[z])
            ingested = rate * available[z]
            loss = grazer_mortality * zoo * zoo
            tend[NNUT + nphy + z, level] = wet * (assimilation * ingested - loss)
            recycled = recycled + loss + (1.0 - assimilation) * ingested
            rates.append(rate)
        for k in range(nphy):
            eaten = prey[0, k] * rates[0]
            for z in range(1, nzoo):
                eaten = eaten + prey[z, k] * rates[z]
            tend[NNUT + k, level] = wet * (tend[NNUT + k, level] - field(NNUT + k) * eaten)
        recycled = wet * recycled
        for j in range(NNUT):
            tend[j, level] = stoichiometry[j] * recycled
        return carry

    lax.fori_loop(0, 1, ecology, 0)

    to_down.wait()
    to_up.wait()
    pad[0:fields, :, FIRST - 2:FIRST, :] = recv_lo[...]
    pad[0:fields, :, FIRST + along:FIRST + along + 2, :] = recv_hi[...]

    def outer_level(level, carry):
        sweep(level, 0, pack_out, 0)
        sweep(level, tiles - 1, pack_out, 1)
        return carry

    lax.fori_loop(0, levels, outer_level, 0)
    late = sides(2, pack_out, left_out, right_out)
    start(late)

    lax.fori_loop(1, levels, ecology, 0)

    @pl.when(jnp.logical_not(has_left))
    def _():
        left_in[...] = jnp.zeros_like(left_in)
        left_out[...] = jnp.zeros_like(left_out)

    @pl.when(jnp.logical_not(has_right))
    def _():
        right_in[...] = jnp.zeros_like(right_in)
        right_out[...] = jnp.zeros_like(right_out)

    for pair in (early, late):
        @pl.when(has_right)
        def _():
            pair[0].wait_send()
            pair[1].wait_recv()

        @pl.when(has_left)
        def _():
            pair[1].wait_send()
            pair[0].wait_recv()

    lane = lax.broadcasted_iota(jnp.int32, left_in.shape[-2:], 1)
    from_left = (lane % GROUP) < 2
    halo[:, 1:tiles - 1] = jnp.where(from_left, left_in[...], right_in[...])
    edge = jnp.where(from_left, left_out[...], right_out[...])
    halo[:, 0] = edge[:, 0]
    halo[:, tiles - 1] = edge[:, 1]


def across_kernel(dims, swept, tend, halo, updated, result, sems):
    count, levels, along = dims
    tiles = along // ROWS
    lane = lax.broadcasted_iota(jnp.int32, (ROWS, LANES), 1)
    low, high = lane < 2, lane >= LANES - 2
    first, final = lane == 0, lane == LANES - 1
    copies = []
    for level in range(levels):
        def step(tile, carry):
            rows = pl.ds(pl.multiple_of(tile * ROWS, ROWS), ROWS)
            packs = [halo[level, tile, g] for g in range(halo.shape[2])]

            def parts(field):
                group, place = divmod(field, PER)
                value = swept[field, level, rows, :]
                ends = pltpu.roll(packs[group], (-GROUP * place - 2) % LANES, 1)
                return value, ends

            def below(value, ends):
                return pltpu.roll(jnp.where(final, ends, value), 1, 1)

            def above(value, ends):
                return pltpu.roll(jnp.where(first, ends, value), LANES - 1, 1)

            flow, flow_ends = parts(count)
            wet, wet_ends = parts(count + 1)
            here = flow * below(wet, wet_ends) * wet
            after = above(flow, flow_ends) * wet * above(wet, wet_ends)
            weights = stencil_weights(here, after)
            for field in range(count):
                value, ends = parts(field)
                before, behind = jnp.where(high, ends, value), jnp.where(low, ends, value)
                total = tend[field, level, rows, :] + value * weights[2]
                total = total + pltpu.roll(before, 2, 1) * weights[0]
                total = total + below(value, ends) * weights[1]
                total = total + above(value, ends) * weights[3]
                total = total + pltpu.roll(behind, LANES - 2, 1) * weights[4]
                result[field, level, rows, :] = total
            return carry

        lax.fori_loop(0, tiles, step, 0)
        copy = pltpu.make_async_copy(result.at[:, level], updated.at[:, level], sems.at[level])
        copy.start()
        copies.append(copy)
    for copy in copies:
        copy.wait()


def shards(
    tracers,
    velocity,
    land_mask,
    sunlight,
    growth_max,
    half_sat,
    light_half,
    graze_max,
    graze_half,
    palatable,
    stoichiometry,
):
    count, levels, along, across = tracers.shape
    assert across == LANES and along % ROWS == 0 and along >= 3 * ROWS
    nphy, nzoo = growth_max.shape[0], graze_max.shape[0]
    fields = count + 2
    groups = -(-fields // PER)
    tiles = along // ROWS
    f32 = jnp.float32
    any_space = pl.BlockSpec(memory_space=pl.ANY)
    vmem = pl.BlockSpec(memory_space=pltpu.VMEM)
    smem = pl.BlockSpec(memory_space=pltpu.SMEM)
    inner_shape = (levels, tiles - 2, groups, ROWS, LANES)
    outer_shape = (levels, 2, groups, ROWS, LANES)
    edge = (fields, levels, 2, LANES)
    swept, tend, halo = pl.pallas_call(
        functools.partial(exchange_kernel, (count, levels, along, nphy, nzoo)),
        out_shape=(
            jax.ShapeDtypeStruct((fields, levels, along, across), f32),
            jax.ShapeDtypeStruct(tracers.shape, f32),
            jax.ShapeDtypeStruct((levels, tiles, groups, ROWS, LANES), f32),
        ),
        in_specs=[any_space] * 4 + [smem] * 7,
        out_specs=(vmem, vmem, vmem),
        scratch_shapes=[
            pltpu.VMEM((count + 3, levels, FIRST + along + ROWS, LANES), f32),
            pltpu.VMEM(land_mask.shape, jnp.int32),
            pltpu.VMEM(sunlight.shape, f32),
            pltpu.VMEM(edge, f32),
            pltpu.VMEM(edge, f32),
            pltpu.VMEM(edge, f32),
            pltpu.VMEM(edge, f32),
            pltpu.VMEM(inner_shape, f32),
            pltpu.VMEM(outer_shape, f32),
            pltpu.VMEM(inner_shape, f32),
            pltpu.VMEM(outer_shape, f32),
            pltpu.VMEM(inner_shape, f32),
            pltpu.VMEM(outer_shape, f32),
            pltpu.SMEM(palatable.shape, f32),
            pltpu.SemaphoreType.DMA((7,)),
            pltpu.SemaphoreType.DMA((2, 2)),
            pltpu.SemaphoreType.DMA((4, 2)),
        ],
        compiler_params=pltpu.CompilerParams(
            collective_id=0, has_side_effects=True, vmem_limit_bytes=24 * 2**20
        ),
        name="exchange",
    )(
        tracers, velocity, land_mask, sunlight, growth_max, half_sat, light_half,
        graze_max, graze_half, palatable, stoichiometry,
    )
    return pl.pallas_call(
        functools.partial(across_kernel, (count, levels, along)),
        out_shape=jax.ShapeDtypeStruct(tracers.shape, f32),
        in_specs=[vmem] * 3,
        out_specs=any_space,
        scratch_shapes=[pltpu.VMEM(tracers.shape, f32), pltpu.SemaphoreType.DMA((levels,))],
        compiler_params=pltpu.CompilerParams(vmem_limit_bytes=24 * 2**20),
        name="across",
    )(swept, tend, halo)


def solution(mesh):
    return jax.shard_map(
        shards,
        mesh=mesh,
        in_specs=(
            P("member", None, "tx", "ty"),
            P(None, None, "tx", "ty"),
            P(None, "tx", "ty"),
            P("tx", "ty"),
            P("member"),
            P("member", None),
            P("member"),
            P("member"),
            P("member"),
            P("member", None),
            P(),
        ),
        out_specs=P("member", None, "tx", "ty"),
        check_vma=False,
    )
```

time: 58.3 us -> 42.2 us (0.72)
  Pallas kernels: 0 us -> 33.1 us
  other arithmetic: 20.5 us -> 0 us
  local copies, waits for them, and re-layouts: 22.6 us -> 8.6 us
  starting transfers between devices: 10.1 us -> 0 us
  matrix products: 4.4 us -> 0 us
    pallas_call x0 -> x2, Pallas kernels: none -> 33.1 us  [the longest x1 17 us: shards(): pl.pallas_call(functools.partial(exchange_kernel, (count, levels, along,...]
    ppermute x4 -> x0, starting transfers between devices: 10.1 us -> none  [the longest x2 7.04 us: extended(): after = lax.ppermute(first, axis, down)]
    slice x8 -> x0, local copies, waits for them, and re-layouts: 8.84 us -> none  [the longest x3 6.08 us: extended(): last = lax.slice_in_dim(array, length - width, length, axis=dim)]
    ppermute x4 -> x0, local copies, waits for them, and re-layouts: 8.02 us -> none  [the longest x2 4.02 us: extended(): before = lax.ppermute(last, axis, up)]
    add x5 -> x0, other arithmetic: 6.62 us -> none  [the longest x2 4.1 us: advect(): face_flux + jnp.abs(transport) * (1.0 / 12.0) * (far_right - 3.0 * near_r...]
    concatenate x4 -> x0, other arithmetic: 4.64 us -> none  [the longest x2 3.11 us: extended(): array = jnp.concatenate([before, array, after], axis=dim)]
    reduce_min x1 -> x0, other arithmetic: 4.58 us -> none  [ecology(): nutrient_limit = jnp.min(saturation, axis=0)]
    dot_general x2 -> x0, matrix products: 4.4 us -> none  [the longest x1 3.21 us: ecology(): jnp.dot(prey_weights.T, grazing_rate, precision=lax.Precision.HIGHEST)]
  transfers between devices with their start and end apart: 4 -> 0, of which waited for: 0 -> 0; matrix products, arithmetic and copies ran while one was open for 39% -> 0% of each run, Pallas kernels for 0% -> 0%
where the time goes in v1:
time: 42.2 us; the launch traced here: 41.7 us
  Pallas kernels  33.1 us (78%)
  local copies, waits for them, and re-layouts  8.6 us (20%)
    pallas_call x1, Pallas kernels, shards(): pl.pallas_call(functools.partial(exchange_kernel, (count, levels, along,...  17 us
    pallas_call x1, Pallas kernels, shards(): pl.pallas_call(functools.partial(across_kernel, (count, levels, along)),...  16.1 us
    unnamed x22, local copies, waits for them, and re-layouts  8.6 us

profile of v1, /device:TPU:1, one launch (start us, length us, event | category | flops | bytes accessed | tf_op | source)
XLA Modules:
  0.0 41.7 jit_solution(5163484157733246200)
XLA Ops:
  0.0 0.0 copy-start
  0.0 1.5 %copy-done = f32[40,3,32,128]{3,2,1,0:T(8,128)S(1)} copy-done((f32[40,3,32,128]{3,2,1,0:T(8,128)S(1)}, f32[40,3,32,128]{3,2,1,0:T(8,128)}, u32[]{:S(2)}) %copy-start) | copy-done | bytes 1966104
  1.5 0.0 copy-start.1
  1.5 0.9 %copy-done.1 = f32[2,3,32,128]{3,2,1,0:T(8,128)S(1)} copy-done((f32[2,3,32,128]{3,2,1,0:T(8,128)S(1)}, f32[2,3,32,128]{3,2,1,0:T(8,128)}, u32[]{:S(2)}) %copy-start.1) | copy-done | bytes 98328
  2.4 0.0 copy-start.2
  2.4 0.8 %copy-done.2 = s32[3,32,128]{2,1,0:T(8,128)S(1)} copy-done((s32[3,32,128]{2,1,0:T(8,128)S(1)}, s32[3,32,128]{2,1,0:T(8,128)}, u32[]{:S(2)}) %copy-start.2) | copy-done | bytes 49176
  3.2 0.0 copy-start.3
  3.2 0.7 %copy-done.3 = f32[32,128]{1,0:T(8,128)S(1)} copy-done((f32[32,128]{1,0:T(8,128)S(1)}, f32[32,128]{1,0:T(8,128)}, u32[]{:S(2)}) %copy-start.3) | copy-done | bytes 16408
  4.0 0.0 copy-start.4
  4.0 0.7 %copy-done.4 = s32[10,26]{1,0:T(8,128)S(1)} copy-done((s32[10,26]{1,0:T(8,128)S(1)}, s32[10,26]{1,0:T(8,128)}, u32[]{:S(2)}) %copy-start.4) | copy-done | bytes 1064
  4.7 0.0 copy-start.5
  4.7 0.7 %copy-done.5 = f32[4,26]{1,0:T(4,128)S(1)} copy-done((f32[4,26]{1,0:T(4,128)S(1)}, f32[4,26]{1,0:T(4,128)}, u32[]{:S(2)}) %copy-start.5) | copy-done | bytes 440
  5.3 0.0 copy-start.6
  5.3 0.7 %copy-done.6 = f32[26]{0:T(128)S(1)} copy-done((f32[26]{0:T(128)S(1)}, f32[26]{0:T(128)}, u32[]{:S(2)}) %copy-start.6) | copy-done | bytes 128
  6.0 0.0 copy-start.7
  6.0 0.7 %copy-done.7 = f32[26]{0:T(128)S(1)} copy-done((f32[26]{0:T(128)S(1)}, f32[26]{0:T(128)}, u32[]{:S(2)}) %copy-start.7) | copy-done | bytes 128
  6.6 0.0 copy-start.8
  6.6 0.7 %copy-done.8 = f32[10]{0:T(128)S(1)} copy-done((f32[10]{0:T(128)S(1)}, f32[10]{0:T(128)}, u32[]{:S(2)}) %copy-start.8) | copy-done | bytes 64
  7.3 0.0 copy-start.9
  7.3 0.7 %copy-done.9 = f32[10]{0:T(128)S(1)} copy-done((f32[10]{0:T(128)S(1)}, f32[10]{0:T(128)}, u32[]{:S(2)}) %copy-start.9) | copy-done | bytes 64
  8.0 0.0 copy-start.10
  8.0 0.7 %copy-done.10 = f32[4]{0:T(128)S(1)} copy-done((f32[4]{0:T(128)S(1)}, f32[4]{0:T(128)}, u32[]{:S(2)}) %copy-start.10) | copy-done | bytes 40
  8.6 17.0 %exchange.1 = (f32[42,3,32,128]{3,2,1,0:T(8,128)S(1)}, f32[40,3,32,128]{3,2,1,0:T(8,128)S(1)}, f32[3,4,2,8,128]{4,3,2,1,0:T(8,128)S(1)}) custom-call(f32[40,3,32,128]{3,2,1,0:T(8,128)S(1)} %copy-done, f32[2,3,32,128]{3,2,1,0:T(8,128)S(1)} %copy-done.1, s32[3,32,128]{2,1,0:T(8,128)S(1)} %copy-done.2, f32[32,128]{1,0:T(8,128)S(1)} %copy-done.3, ...), custom_call_target="tpu_custom_call" | custom-call | tf_op jit(solution)/shard_map/exchange/pallas_call | solution.py:348
  25.6 16.1 %across.1 = f32[40,3,32,128]{3,2,1,0:T(8,128)} custom-call(f32[42,3,32,128]{3,2,1,0:T(8,128)S(1)} %get-tuple-element.8.swept, f32[40,3,32,128]{3,2,1,0:T(8,128)S(1)} %get-tuple-element.9.tend, f32[3,4,2,8,128]{4,3,2,1,0:T(8,128)S(1)} %get-tuple-element.10.halo), custom_call_target="tpu_custom_call" | custom-call | tf_op jit(solution)/shard_map/across/pallas_call | solution.py:384
Async XLA Ops:
  0.0 1.5 %copy-start = (f32[40,3,32,128]{3,2,1,0:T(8,128)S(1)}, f32[40,3,32,128]{3,2,1,0:T(8,128)}, u32[]{:S(2)}) copy-start(f32[40,3,32,128]{3,2,1,0:T(8,128)} %tracers.1) | copy-start | bytes 5898244
  1.5 0.9 %copy-start.1 = (f32[2,3,32,128]{3,2,1,0:T(8,128)S(1)}, f32[2,3,32,128]{3,2,1,0:T(8,128)}, u32[]{:S(2)}) copy-start(f32[2,3,32,128]{3,2,1,0:T(8,128)} %velocity.1) | copy-start | bytes 294916
  2.4 0.8 %copy-start.2 = (s32[3,32,128]{2,1,0:T(8,128)S(1)}, s32[3,32,128]{2,1,0:T(8,128)}, u32[]{:S(2)}) copy-start(s32[3,32,128]{2,1,0:T(8,128)} %land_mask.1) | copy-start | bytes 147460
  3.2 0.7 %copy-start.3 = (f32[32,128]{1,0:T(8,128)S(1)}, f32[32,128]{1,0:T(8,128)}, u32[]{:S(2)}) copy-start(f32[32,128]{1,0:T(8,128)} %sunlight.1) | copy-start | bytes 49156
  4.0 0.7 %copy-start.4 = (s32[10,26]{1,0:T(8,128)S(1)}, s32[10,26]{1,0:T(8,128)}, u32[]{:S(2)}) copy-start(s32[10,26]{1,0:T(8,128)} %palatable.1) | copy-start | bytes 3124
  4.7 0.7 %copy-start.5 = (f32[4,26]{1,0:T(4,128)S(1)}, f32[4,26]{1,0:T(4,128)}, u32[]{:S(2)}) copy-start(f32[4,26]{1,0:T(4,128)} %half_sat.1) | copy-start | bytes 1252
  5.3 0.7 %copy-start.6 = (f32[26]{0:T(128)S(1)}, f32[26]{0:T(128)}, u32[]{:S(2)}) copy-start(f32[26]{0:T(128)} %growth_max.1) | copy-start | bytes 316
  6.0 0.7 %copy-start.7 = (f32[26]{0:T(128)S(1)}, f32[26]{0:T(128)}, u32[]{:S(2)}) copy-start(f32[26]{0:T(128)} %light_half.1) | copy-start | bytes 316
  6.6 0.7 %copy-start.8 = (f32[10]{0:T(128)S(1)}, f32[10]{0:T(128)}, u32[]{:S(2)}) copy-start(f32[10]{0:T(128)} %graze_max.1) | copy-start | bytes 124
  7.3 0.7 %copy-start.9 = (f32[10]{0:T(128)S(1)}, f32[10]{0:T(128)}, u32[]{:S(2)}) copy-start(f32[10]{0:T(128)} %graze_half.1) | copy-start | bytes 124
  8.0 0.7 %copy-start.10 = (f32[4]{0:T(128)S(1)}, f32[4]{0:T(128)}, u32[]{:S(2)}) copy-start(f32[4]{0:T(128)} %stoichiometry.1) | copy-start | bytes 52

commit v2 on v1

--- a/solution.py
+++ b/solution.py
@@ -18,6 +18,7 @@
 FIRST = 8
 GROUP = 4
 PER = LANES // GROUP
+BATCH = 8
 MESH = pl.DeviceIdType.MESH
 
 
@@ -40,16 +41,11 @@
     velocity,
     land_mask,
     sunlight,
-    growth_max,
-    half_sat,
-    light_half,
-    graze_max,
-    graze_half,
-    palatable,
-    stoichiometry,
-    swept,
-    tend,
-    halo,
+    *refs,
+):
+    sources, (swept, tend, halo), tables, buffers = refs[:7], refs[7:10], refs[10:17], refs[17:]
+    growth_max, half_sat, light_half, graze_max, graze_half, palatable, stoichiometry = tables
+    (
     pad,
     mask_buf,
     sun_buf,
@@ -67,7 +63,7 @@
     load_sems,
     row_sems,
     col_sems,
-):
+    ) = buffers
     count, levels, along, nphy, nzoo = dims
     fields = count + 2
     tiles = along // ROWS
@@ -94,6 +90,7 @@
         load(5, velocity.at[1], pad.at[count + 2, :, pl.ds(FIRST, along), :]),
         load(6, sunlight, sun_buf),
     ]
+    small = [load(7 + i, src, dst) for i, (src, dst) in enumerate(zip(sources, tables))]
 
     barrier = pltpu.get_barrier_semaphore()
     for target in ({"tx": up}, {"tx": down}, {"ty": right}, {"ty": left}):
@@ -104,6 +101,8 @@
             prey[z, k] = palatable[z, k].astype(jnp.float32)
         return carry
 
+    for copy in small:
+        copy.wait()
     lax.fori_loop(0, nzoo, to_float, 0)
 
     loads[0].wait()
@@ -141,22 +140,28 @@
         after = at(count, 1) * wet * at(count + 1, 1)
         weights = stencil_weights(here, after)
         packed = [None] * (-(-fields // PER))
-        for field in range(fields):
-            if field < count:
-                value = at(field, -2) * weights[0]
-                for shift in range(-1, 3):
-                    value = value + at(field, shift) * weights[shift + 2]
-            elif field == count:
-                value = at(count + 2, 0)
-            else:
-                value = wet
-            swept[field, level, pl.ds(tile * ROWS, ROWS), :] = value
-            group, place = divmod(field, PER)
-            turned = pltpu.roll(value, (GROUP * place + 2) % LANES, 1)
-            if place == 0:
-                packed[group] = turned
-            else:
-                packed[group] = jnp.where(lane_group == place, turned, packed[group])
+        for begin in range(0, fields, BATCH):
+            batch = range(begin, min(begin + BATCH, fields))
+            values = []
+            for field in batch:
+                if field < count:
+                    value = at(field, -2) * weights[0]
+                    for shift in range(-1, 3):
+                        value = value + at(field, shift) * weights[shift + 2]
+                elif field == count:
+                    value = at(count + 2, 0)
+                else:
+                    value = wet
+                values.append(value)
+            for field, value in zip(batch, values):
+                group, place = divmod(field, PER)
+                turned = pltpu.roll(value, (GROUP * place + 2) % LANES, 1)
+                if place == 0:
+                    packed[group] = turned
+                else:
+                    packed[group] = jnp.where(lane_group == place, turned, packed[group])
+            for field, value in zip(batch, values):
+                swept[field, level, pl.ds(tile * ROWS, ROWS), :] = value
         for group, value in enumerate(packed):
             pack[level, spot, group] = value
 
@@ -300,15 +305,21 @@
             here = flow * below(wet, wet_ends) * wet
             after = above(flow, flow_ends) * wet * above(wet, wet_ends)
             weights = stencil_weights(here, after)
-            for field in range(count):
-                value, ends = parts(field)
-                before, behind = jnp.where(high, ends, value), jnp.where(low, ends, value)
-                total = tend[field, level, rows, :] + value * weights[2]
-                total = total + pltpu.roll(before, 2, 1) * weights[0]
-                total = total + below(value, ends) * weights[1]
-                total = total + above(value, ends) * weights[3]
-                total = total + pltpu.roll(behind, LANES - 2, 1) * weights[4]
-                result[field, level, rows, :] = total
+            for begin in range(0, count, BATCH):
+                batch = range(begin, min(begin + BATCH, count))
+                pairs = [parts(field) for field in batch]
+                far_before = [pltpu.roll(jnp.where(high, e, v), 2, 1) for v, e in pairs]
+                near_before = [below(v, e) for v, e in pairs]
+                near_behind = [above(v, e) for v, e in pairs]
+                far_behind = [pltpu.roll(jnp.where(low, e, v), LANES - 2, 1) for v, e in pairs]
+                totals = []
+                for i, field in enumerate(batch):
+                    total = tend[field, level, rows, :] + pairs[i][0] * weights[2]
+                    total = total + far_before[i] * weights[0] + near_before[i] * weights[1]
+                    total = total + near_behind[i] * weights[3] + far_behind[i] * weights[4]
+                    totals.append(total)
+                for i, field in enumerate(batch):
+                    result[field, level, rows, :] = totals[i]
             return carry
 
         lax.fori_loop(0, tiles, step, 0)
@@ -340,8 +351,9 @@
     tiles = along // ROWS
     f32 = jnp.float32
     any_space = pl.BlockSpec(memory_space=pl.ANY)
+    hbm = pl.BlockSpec(memory_space=pltpu.HBM)
     vmem = pl.BlockSpec(memory_space=pltpu.VMEM)
-    smem = pl.BlockSpec(memory_space=pltpu.SMEM)
+    small = (growth_max, half_sat, light_half, graze_max, graze_half, palatable, stoichiometry)
     inner_shape = (levels, tiles - 2, groups, ROWS, LANES)
     outer_shape = (levels, 2, groups, ROWS, LANES)
     edge = (fields, levels, 2, LANES)
@@ -352,9 +364,9 @@
             jax.ShapeDtypeStruct(tracers.shape, f32),
             jax.ShapeDtypeStruct((levels, tiles, groups, ROWS, LANES), f32),
         ),
-        in_specs=[any_space] * 4 + [smem] * 7,
+        in_specs=[hbm] * 11,
         out_specs=(vmem, vmem, vmem),
-        scratch_shapes=[
+        scratch_shapes=[pltpu.SMEM(x.shape, x.dtype) for x in small] + [
             pltpu.VMEM((count + 3, levels, FIRST + along + ROWS, LANES), f32),
             pltpu.VMEM(land_mask.shape, jnp.int32),
             pltpu.VMEM(sunlight.shape, f32),
@@ -369,7 +381,7 @@
             pltpu.VMEM(inner_shape, f32),
             pltpu.VMEM(outer_shape, f32),
             pltpu.SMEM(palatable.shape, f32),
-            pltpu.SemaphoreType.DMA((7,)),
+            pltpu.SemaphoreType.DMA((14,)),
             pltpu.SemaphoreType.DMA((2, 2)),
             pltpu.SemaphoreType.DMA((4, 2)),
         ],
@@ -377,10 +389,10 @@
             collective_id=0, has_side_effects=True, vmem_limit_bytes=24 * 2**20
         ),
         name="exchange",
-    )(
-        tracers, velocity, land_mask, sunlight, growth_max, half_sat, light_half,
-        graze_max, graze_half, palatable, stoichiometry,
-    )
+    )(*[
+        pltpu.with_memory_space_constraint(x, pltpu.HBM)
+        for x in (tracers, velocity, land_mask, sunlight) + small
+    ])
     return pl.pallas_call(
         functools.partial(across_kernel, (count, levels, along)),
         out_shape=jax.ShapeDtypeStruct(tracers.shape, f32),

time: 42.2 us -> 23.5 us (0.56)
  Pallas kernels: 33.1 us -> 23.3 us
  local copies, waits for them, and re-layouts: 8.6 us -> 0 us
    pallas_call x1, Pallas kernels: 16.1 us -> 6.8 us  [shards(): pl.pallas_call(functools.partial(across_kernel, (count, levels, along)),...]
    unnamed x22 -> x0, local copies, waits for them, and re-layouts: 8.6 us -> none
    pallas_call x1, Pallas kernels: 17 us -> 16.5 us  [shards(): pl.pallas_call(functools.partial(exchange_kernel, (count, levels, along,...]
where the time goes in v2:
time: 23.5 us; the launch traced here: 23.3 us
  Pallas kernels  23.3 us (99%)
    pallas_call x1, Pallas kernels, shards(): pl.pallas_call(functools.partial(exchange_kernel, (count, levels, along,...  16.5 us
    pallas_call x1, Pallas kernels, shards(): pl.pallas_call(functools.partial(across_kernel, (count, levels, along)),...  6.8 us

profile of v2, /device:TPU:1, one launch (start us, length us, event | category | flops | bytes accessed | tf_op | source)
XLA Modules:
  0.0 23.3 jit_solution(14784179412887007019)
XLA Ops:
  0.0 16.5 %exchange.1 = (f32[42,3,32,128]{3,2,1,0:T(8,128)S(1)}, f32[40,3,32,128]{3,2,1,0:T(8,128)S(1)}, f32[3,4,2,8,128]{4,3,2,1,0:T(8,128)S(1)}) custom-call(f32[40,3,32,128]{3,2,1,0:T(8,128)} %tracers.1, f32[2,3,32,128]{3,2,1,0:T(8,128)} %velocity.1, s32[3,32,128]{2,1,0:T(8,128)} %land_mask.1, f32[32,128]{1,0:T(8,128)} %sunlight.1, f32[26]{0:T(128)} %refs_0_.1, ...), custom_call_target="tpu_custom_call" | custom-call | tf_op jit(solution)/shard_map/exchange/pallas_call | solution.py:360
  16.5 6.8 %across.1 = f32[40,3,32,128]{3,2,1,0:T(8,128)} custom-call(f32[42,3,32,128]{3,2,1,0:T(8,128)S(1)} %get-tuple-element.8.swept, f32[40,3,32,128]{3,2,1,0:T(8,128)S(1)} %get-tuple-element.9.tend, f32[3,4,2,8,128]{4,3,2,1,0:T(8,128)S(1)} %get-tuple-element.10.halo), custom_call_target="tpu_custom_call" | custom-call | tf_op jit(solution)/shard_map/across/pallas_call | solution.py:396

commit v3 on v2

--- a/solution.py
+++ b/solution.py
@@ -229,7 +229,7 @@
             tend[j, level] = stoichiometry[j] * recycled
         return carry
 
-    lax.fori_loop(0, 1, ecology, 0)
+    lax.fori_loop(0, levels, ecology, 0)
 
     to_down.wait()
     to_up.wait()
@@ -245,8 +245,6 @@
     late = sides(2, pack_out, left_out, right_out)
     start(late)
 
-    lax.fori_loop(1, levels, ecology, 0)
-
     @pl.when(jnp.logical_not(has_left))
     def _():
         left_in[...] = jnp.zeros_like(left_in)
@@ -257,7 +255,7 @@
         right_in[...] = jnp.zeros_like(right_in)
         right_out[...] = jnp.zeros_like(right_out)
 
-    for pair in (early, late):
+    def finish(pair):
         @pl.when(has_right)
         def _():
             pair[0].wait_send()
@@ -268,62 +266,79 @@
             pair[1].wait_send()
             pair[0].wait_recv()
 
-    lane = lax.broadcasted_iota(jnp.int32, left_in.shape[-2:], 1)
+    finish(early)
+    lane = lax.broadcasted_iota(jnp.int32, (ROWS, LANES), 1)
     from_left = (lane % GROUP) < 2
-    halo[:, 1:tiles - 1] = jnp.where(from_left, left_in[...], right_in[...])
-    edge = jnp.where(from_left, left_out[...], right_out[...])
-    halo[:, 0] = edge[:, 0]
-    halo[:, tiles - 1] = edge[:, 1]
+
+    def across_level(level, carry):
+        for tile in range(1, tiles - 1):
+            packs = [
+                jnp.where(from_left, left_in[level, tile - 1, g], right_in[level, tile - 1, g])
+                for g in range(halo.shape[2])
+            ]
+            across_tile(count, level, tile, packs, swept, tend, tend)
+        return carry
+
+    lax.fori_loop(0, levels, across_level, 0)
+    finish(late)
+    halo[...] = jnp.where(from_left, left_out[...], right_out[...])
+
+
+def across_tile(count, level, tile, packs, swept, tend, result):
+    lane = lax.broadcasted_iota(jnp.int32, (ROWS, LANES), 1)
+    low, high = lane < 2, lane >= LANES - 2
+    first, final = lane == 0, lane == LANES - 1
+    rows = pl.ds(tile * ROWS, ROWS)
+
+    def parts(field):
+        group, place = divmod(field, PER)
+        value = swept[field, level, rows, :]
+        ends = pltpu.roll(packs[group], (-GROUP * place - 2) % LANES, 1)
+        return value, ends
+
+    def below(value, ends):
+        return pltpu.roll(jnp.where(final, ends, value), 1, 1)
+
+    def above(value, ends):
+        return pltpu.roll(jnp.where(first, ends, value), LANES - 1, 1)
+
+    flow, flow_ends = parts(count)
+    wet, wet_ends = parts(count + 1)
+    here = flow * below(wet, wet_ends) * wet
+    after = above(flow, flow_ends) * wet * above(wet, wet_ends)
+    weights = stencil_weights(here, after)
+    for begin in range(0, count, BATCH):
+        batch = range(begin, min(begin + BATCH, count))
+        pairs = [parts(field) for field in batch]
+        far_before = [pltpu.roll(jnp.where(high, e, v), 2, 1) for v, e in pairs]
+        near_before = [below(v, e) for v, e in pairs]
+        near_behind = [above(v, e) for v, e in pairs]
+        far_behind = [pltpu.roll(jnp.where(low, e, v), LANES - 2, 1) for v, e in pairs]
+        totals = []
+        for i, field in enumerate(batch):
+            total = tend[field, level, rows, :] + pairs[i][0] * weights[2]
+            total = total + far_before[i] * weights[0] + near_before[i] * weights[1]
+            total = total + near_behind[i] * weights[3] + far_behind[i] * weights[4]
+            totals.append(total)
+        for i, field in enumerate(batch):
+            result[field, level, rows, :] = totals[i]
 
 
 def across_kernel(dims, swept, tend, halo, updated, result, sems):
     count, levels, along = dims
     tiles = along // ROWS
-    lane = lax.broadcasted_iota(jnp.int32, (ROWS, LANES), 1)
-    low, high = lane < 2, lane >= LANES - 2
-    first, final = lane == 0, lane == LANES - 1
-    copies = []
-    for level in range(levels):
-        def step(tile, carry):
-            rows = pl.ds(pl.multiple_of(tile * ROWS, ROWS), ROWS)
-            packs = [halo[level, tile, g] for g in range(halo.shape[2])]
-
-            def parts(field):
-                group, place = divmod(field, PER)
-                value = swept[field, level, rows, :]
-                ends = pltpu.roll(packs[group], (-GROUP * place - 2) % LANES, 1)
-                return value, ends
-
-            def below(value, ends):
-                return pltpu.roll(jnp.where(final, ends, value), 1, 1)
-
-            def above(value, ends):
-                return pltpu.roll(jnp.where(first, ends, value), LANES - 1, 1)
-
-            flow, flow_ends = parts(count)
-            wet, wet_ends = parts(count + 1)
-            here = flow * below(wet, wet_ends) * wet
-            after = above(flow, flow_ends) * wet * above(wet, wet_ends)
-            weights = stencil_weights(here, after)
-            for begin in range(0, count, BATCH):
-                batch = range(begin, min(begin + BATCH, count))
-                pairs = [parts(field) for field in batch]
-                far_before = [pltpu.roll(jnp.where(high, e, v), 2, 1) for v, e in pairs]
-                near_before = [below(v, e) for v, e in pairs]
-                near_behind = [above(v, e) for v, e in pairs]
-                far_behind = [pltpu.roll(jnp.where(low, e, v), LANES - 2, 1) for v, e in pairs]
-                totals = []
-                for i, field in enumerate(batch):
-                    total = tend[field, level, rows, :] + pairs[i][0] * weights[2]
-                    total = total + far_before[i] * weights[0] + near_before[i] * weights[1]
-                    total = total + near_behind[i] * weights[3] + far_behind[i] * weights[4]
-                    totals.append(total)
-                for i, field in enumerate(batch):
-                    result[field, level, rows, :] = totals[i]
+    inner = pl.ds(ROWS, along - 2 * ROWS)
+    copies = [pltpu.make_async_copy(tend.at[:, :, inner, :], updated.at[:, :, inner, :], sems.at[0])]
+    copies[0].start()
+    for spot, tile in enumerate((0, tiles - 1)):
+        def step(level, carry):
+            packs = [halo[level, spot, g] for g in range(halo.shape[2])]
+            across_tile(count, level, tile, packs, swept, tend, result)
             return carry
 
-        lax.fori_loop(0, tiles, step, 0)
-        copy = pltpu.make_async_copy(result.at[:, level], updated.at[:, level], sems.at[level])
+        lax.fori_loop(0, levels, step, 0)
+        rows = pl.ds(tile * ROWS, ROWS)
+        copy = pltpu.make_async_copy(result.at[:, :, rows, :], updated.at[:, :, rows, :], sems.at[spot + 1])
         copy.start()
         copies.append(copy)
     for copy in copies:
@@ -362,7 +377,7 @@
         out_shape=(
             jax.ShapeDtypeStruct((fields, levels, along, across), f32),
             jax.ShapeDtypeStruct(tracers.shape, f32),
-            jax.ShapeDtypeStruct((levels, tiles, groups, ROWS, LANES), f32),
+            jax.ShapeDtypeStruct(outer_shape, f32),
         ),
         in_specs=[hbm] * 11,
         out_specs=(vmem, vmem, vmem),
@@ -398,7 +413,7 @@
         out_shape=jax.ShapeDtypeStruct(tracers.shape, f32),
         in_specs=[vmem] * 3,
         out_specs=any_space,
-        scratch_shapes=[pltpu.VMEM(tracers.shape, f32), pltpu.SemaphoreType.DMA((levels,))],
+        scratch_shapes=[pltpu.VMEM(tracers.shape, f32), pltpu.SemaphoreType.DMA((3,))],
         compiler_params=pltpu.CompilerParams(vmem_limit_bytes=24 * 2**20),
         name="across",
     )(swept, tend, halo)

time: 23.5 us -> 21.2 us (0.902)
  the two profiles are of different devices: /device:TPU:1 before, /device:TPU:0 now
where the time goes in v3:
time: 21.2 us; the launch traced here: 21 us
  Pallas kernels  21 us (99%)
    pallas_call x1, Pallas kernels, shards(): pl.pallas_call(functools.partial(exchange_kernel, (count, levels, along,...  17.2 us
    pallas_call x1, Pallas kernels, shards(): pl.pallas_call(functools.partial(across_kernel, (count, levels, along)),...  3.78 us

profile of v3, /device:TPU:0, one launch (start us, length us, event | category | flops | bytes accessed | tf_op | source)
XLA Modules:
  0.0 21.0 jit_solution(7860125425672112912)
XLA Ops:
  0.0 17.2 %exchange.1 = (f32[42,3,32,128]{3,2,1,0:T(8,128)S(1)}, f32[40,3,32,128]{3,2,1,0:T(8,128)S(1)}, f32[3,2,2,8,128]{4,3,2,1,0:T(8,128)S(1)}) custom-call(f32[40,3,32,128]{3,2,1,0:T(8,128)} %tracers.1, f32[2,3,32,128]{3,2,1,0:T(8,128)} %velocity.1, s32[3,32,128]{2,1,0:T(8,128)} %land_mask.1, f32[32,128]{1,0:T(8,128)} %sunlight.1, f32[26]{0:T(128)} %refs_0_.1, ...), custom_call_target="tpu_custom_call" | custom-call | tf_op jit(solution)/shard_map/exchange/pallas_call | solution.py:375
  17.2 3.8 %across.1 = f32[40,3,32,128]{3,2,1,0:T(8,128)} custom-call(f32[42,3,32,128]{3,2,1,0:T(8,128)S(1)} %get-tuple-element.8.swept, f32[40,3,32,128]{3,2,1,0:T(8,128)S(1)} %get-tuple-element.9.tend, f32[3,2,2,8,128]{4,3,2,1,0:T(8,128)S(1)} %get-tuple-element.10.halo), custom_call_target="tpu_custom_call" | custom-call | tf_op jit(solution)/shard_map/across/pallas_call | solution.py:411
